TPU v7x, 32 devices: a whole 2x2x4 slice. The times are simulated.
32 devices in a mesh: batch: 8 (over z, y), group: 4 (over x, core).
Axes of the slice: x: 2, y: 2, z: 4, core: 2. Of those that a mesh axis runs over, the one named last changes fastest.
Arguments:
- samples_in: float32 [2048, 1024], P('batch', 'group'), may hold values from -8 to 8, as said below
- second_samples_in: float32 [2048, 1024], P('batch', 'group'), may hold values from -8 to 8, as said below
Outputs:
- standard: float32 [2048, 1024], P(None, ('group', 'batch'))
- second_standard: float32 [2048, 1024], P(None, ('group', 'batch'))
Inputs may be any that keep to these rules, and one draw needn't show every extreme that they name: samples_in holds numbers from -8 to 8. second_samples_in holds numbers from -8 to 8.
All inputs are finite; a program needn't handle non-finite values.
Results may differ from a plain program's by a relative error of at most 0.0003.
Values sent between devices are 32-bit elements.
A program may use at most 64 MiB of HBM per device.

v0:
```python
import jax
import jax.numpy as jnp
from jax import lax
from jax.sharding import PartitionSpec as P


def shards(samples_in, second_samples_in):
    moved_samples_in, moved_second_samples_in = (
        lax.all_to_all(samples_in, "batch", split_axis=1, concat_axis=0, tiled=True),
        lax.all_to_all(second_samples_in, "batch", split_axis=1, concat_axis=0, tiled=True),
    )
    wide_standard = moved_samples_in.astype(jnp.float32)
    low_standard = jnp.mean(jnp.minimum(wide_standard, 1.0), axis=0)
    high_standard = jnp.mean(jnp.maximum(wide_standard, 1.0), axis=0)
    standard = (wide_standard - low_standard) / (high_standard - low_standard + 0.1)
    wide_second_standard = moved_second_samples_in.astype(jnp.float32)
    low_second_standard = jnp.mean(jnp.minimum(wide_second_standard, 1.0), axis=0)
    high_second_standard = jnp.mean(jnp.maximum(wide_second_standard, 1.0), axis=0)
    second_standard = (wide_second_standard - low_second_standard) / (
        high_second_standard - low_second_standard + 0.1
    )
    return (standard, second_standard)


def solution(mesh):
    placed = (P("batch", "group"), P("batch", "group"))
    return jax.shard_map(
        shards,
        mesh=mesh,
        in_specs=placed,
        out_specs=(P(None, ("group", "batch")), P(None, ("group", "batch"))),
        check_vma=False,
    )
```

profile of v0, /device:TPU:0, one launch (start us, length us, event | category | flops | bytes accessed | tf_op | source)
XLA Modules:
  0.0 33.0 jit_solution(18137346310307932450)
XLA Ops:
  0.6 1.8 %copy.8 = f32[256,256]{0,1:T(8,128)} copy(f32[256,256]{1,0:T(8,128)} %param.2) | data formatting | bytes 524288 | tf_op args[0]
  2.4 0.0 copy-start
  2.4 7.5 %all-to-all-start = ((f32[256,8,32]{0,2,1:T(8,128)}), f32[256,8,32]{0,2,1:T(8,128)S(1)}, u32[]{:S(2)}, u32[]{:S(2)}) async-start(f32[256,8,32]{0,2,1:T(8,128)} %bitcast), calls=%async_computation | async-start | bytes 524288 | tf_op jit(solution)/shard_map/all_to_all | solution.py:9
  9.9 0.0 copy-done
  9.9 0.8 %copy.10 = f32[256,256]{0,1:T(8,128)} copy(f32[256,256]{1,0:T(8,128)S(1)} %copy-done) | data formatting | bytes 524288 | tf_op args[1]
  10.7 8.1 %all-to-all-done = f32[256,8,32]{0,2,1:T(8,128)S(1)} async-done(((f32[256,8,32]{0,2,1:T(8,128)}), f32[256,8,32]{0,2,1:T(8,128)S(1)}, u32[]{:S(2)}, u32[]{:S(2)}) %all-to-all-start) | async-done | bytes 262176 | tf_op jit(solution)/shard_map/all_to_all | solution.py:9
  18.8 3.6 %all-to-all-start.1 = ((f32[256,8,32]{0,2,1:T(8,128)}), f32[256,8,32]{0,2,1:T(8,128)S(1)}, u32[]{:S(2)}, u32[]{:S(2)}) async-start(f32[256,8,32]{0,2,1:T(8,128)} %bitcast.2), calls=%async_computation.1 | async-start | bytes 524288 | tf_op jit(solution)/shard_map/all_to_all | solution.py:10
  22.5 9.3 %all-to-all-done.1 = f32[256,8,32]{0,2,1:T(8,128)S(1)} async-done(((f32[256,8,32]{0,2,1:T(8,128)}), f32[256,8,32]{0,2,1:T(8,128)S(1)}, u32[]{:S(2)}, u32[]{:S(2)}) %all-to-all-start.1) | async-done | bytes 262176 | tf_op jit(solution)/shard_map/all_to_all | solution.py:10
  31.7 0.1 fusion.3
  31.9 0.1 fusion.1
  32.1 0.9 %subtract_divide_fusion = (f32[2048,32]{0,1:T(8,128)}, f32[2048,32]{0,1:T(8,128)}) fusion(f32[2048,32]{0,1:T(8,128)S(1)} %bitcast.23, f32[32]{0:T(128)S(1)} %get-tuple-element.7, f32[32]{0:T(128)S(1)} %get-tuple-element.6, f32[32]{0:T(128)S(1)} %get-tuple-element.9, f32[2048,32]{0,1:T(8,128)S(1)} %bitcast.22, f32[32]{0:T(128)S(1)} %get-tuple-element.8), kind=kLoop, calls=%fused_computation.8 | loop fusion | flops 262144 | bytes 1049088 | tf_op jit(solution)/shard_map/div | solution.py:19
  (4 shorter events, 0.1 us)
Async XLA Ops:
  2.4 7.5 %copy-start = (f32[256,256]{1,0:T(8,128)S(1)}, f32[256,256]{1,0:T(8,128)}, u32[]{:S(2)}) copy-start(f32[256,256]{1,0:T(8,128)} %param.3) | copy-start | bytes 786436
  2.4 16.4 %all-to-all-start = ((f32[256,8,32]{0,2,1:T(8,128)}), f32[256,8,32]{0,2,1:T(8,128)S(1)}, u32[]{:S(2)}, u32[]{:S(2)}) async-start(f32[256,8,32]{0,2,1:T(8,128)} %bitcast), calls=%async_computation | async-start | bytes 524288 | tf_op jit(solution)/shard_map/all_to_all | solution.py:9
  18.8 12.9 %all-to-all-start.1 = ((f32[256,8,32]{0,2,1:T(8,128)}), f32[256,8,32]{0,2,1:T(8,128)S(1)}, u32[]{:S(2)}, u32[]{:S(2)}) async-start(f32[256,8,32]{0,2,1:T(8,128)} %bitcast.2), calls=%async_computation.1 | async-start | bytes 524288 | tf_op jit(solution)/shard_map/all_to_all | solution.py:10
where the time goes:
time: 33.3 us; the launch traced here: 33 us
  waiting for transfers between devices  17.3 us (52%)
  starting transfers between devices  11.1 us (33%)
  local copies, waits for them, and re-layouts  2.66 us (8%)
  other arithmetic  1.22 us (4%)
  between operations  0.65 us (2%)
    all_to_all x1, waiting for transfers between devices, shards(): lax.all_to_all(second_samples_in, 'batch', split_axis=1, concat_axis=0, t...  9.25 us
    all_to_all x1, waiting for transfers between devices, shards(): lax.all_to_all(samples_in, 'batch', split_axis=1, concat_axis=0, tiled=True)  8.07 us
    all_to_all x1, starting transfers between devices, shards(): lax.all_to_all(samples_in, 'batch', split_axis=1, concat_axis=0, tiled=True)  7.47 us
    all_to_all x1, starting transfers between devices, shards(): lax.all_to_all(second_samples_in, 'batch', split_axis=1, concat_axis=0, t...  3.63 us
    unnamed x4, local copies, waits for them, and re-layouts  2.63 us
    div x1, other arithmetic, shards(): (wide_second_standard - low_second_standard) / (high_second_standard - lo...  0.91 us
  transfers between devices with their start and end apart: 2, of which 2 were waited for; matrix products, arithmetic and copies ran while one was open for 3% of the time, Pallas kernels for 0%

commit v1 on v0

v1 whole, which is shorter than its diff:
```python
import functools

import jax
import jax.numpy as jnp
from jax import lax
from jax.experimental import pallas as pl
from jax.experimental.pallas import tpu as pltpu
from jax.sharding import PartitionSpec as P

MESH = pl.DeviceIdType.MESH
LANES = 128


def loop(count, body, init):
    if count <= 8:
        for step in range(count):
            init = body(step, init)
        return init
    return lax.fori_loop(0, count, body, init)


def kernel(n, first_hbm, second_hbm, first_out, second_out, raw, turned, got, load_sem, send_sem, recv_sem):
    ins = (first_hbm, second_hbm)
    outs = (first_out, second_out)
    rows, width = first_hbm.shape
    block = width // n
    half = n // 2
    span = half * block
    me = lax.axis_index("batch")
    mine, place = me // half, me % half
    sides = ((mine + 1) % 2, mine)

    def load(side, a):
        start = pl.multiple_of(sides[side] * span, span)
        return pltpu.make_async_copy(
            ins[a].at[:, pl.ds(start, span)], raw.at[a, side], load_sem.at[a, side]
        )

    for side in range(2):
        for a in range(2):
            load(side, a).start()

    barrier = pltpu.get_barrier_semaphore()

    def greet(step, carry):
        pl.semaphore_signal(
            barrier, inc=1, device_id={"batch": (me + 1 + step) % n}, device_id_type=MESH
        )
        return carry

    loop(n - 1, greet, 0)

    def send(side, a, step):
        spot = (place + step) % half
        return pltpu.make_async_remote_copy(
            src_ref=turned.at[a, side, spot],
            dst_ref=got.at[a, me],
            send_sem=send_sem.at[a, side, step],
            recv_sem=recv_sem.at[a, me],
            device_id={"batch": sides[side] * half + spot},
            device_id_type=MESH,
        )

    def arrival(side, a, step):
        source = sides[side] * half + (place - step + half) % half
        copy = pltpu.make_async_remote_copy(
            src_ref=turned.at[a, side, 0],
            dst_ref=got.at[a, source],
            send_sem=send_sem.at[a, side, step],
            recv_sem=recv_sem.at[a, source],
            device_id={"batch": source},
            device_id_type=MESH,
        )
        return source, copy

    greeted = False
    for side in range(2):
        for a in range(2):
            load(side, a).wait()
            for start in range(0, span, LANES):
                tile = raw[a, side, :, start : start + LANES].T
                turned[a, side, start // block : (start + LANES) // block] = tile.reshape(
                    LANES // block, block, rows
                )
            if not greeted:
                pl.semaphore_wait(barrier, n - 1)
                greeted = True

            def push(step, carry, side=side, a=a):
                send(side, a, step + side).start()
                return carry

            loop(half - side, push, 0)

    def add(sums, values):
        low, high = sums
        for start in range(0, rows, LANES):
            part = values[:, start : start + LANES]
            low += jnp.minimum(part, 1.0)
            high += jnp.maximum(part, 1.0)
        return low, high

    zero = jnp.zeros((block, LANES), jnp.float32)
    sums = []
    for a in range(2):
        own = turned[a, 1, place]
        got[a, me] = own
        sums.append(add((zero, zero), own))
    for side in range(2):
        for a in range(2):

            def take(step, carry, side=side, a=a):
                source, copy = arrival(side, a, step + side)
                copy.wait_recv()
                return add(carry, got[a, source])

            sums[a] = loop(half - side, take, sums[a])

    for a in range(2):
        low, high = (jnp.sum(s, axis=1, keepdims=True) / (n * rows) for s in sums[a])
        scale = 1.0 / (high - low + 0.1)
        low = jnp.broadcast_to(low, (block, rows))
        scale = jnp.broadcast_to(scale, (block, rows))
        out = outs[a]

        def rescale(source, carry, a=a, out=out, low=low, scale=scale):
            start = source * rows
            if not isinstance(start, int):
                start = pl.multiple_of(start, LANES)
            out[:, pl.ds(start, rows)] = (got[a, source] - low) * scale
            return carry

        loop(n, rescale, 0)

    for side in range(2):
        for a in range(2):

            def drain(step, carry, side=side, a=a):
                send(side, a, step + side).wait_send()
                return carry

            loop(half - side, drain, 0)


def solution(mesh):
    n = mesh.shape["batch"]

    def shards(samples_in, second_samples_in):
        rows, width = samples_in.shape
        block = width // n
        half = n // 2
        out = jax.ShapeDtypeStruct((block, n * rows), jnp.float32)
        first, second = pl.pallas_call(
            functools.partial(kernel, n),
            out_shape=(out, out),
            in_specs=[pl.BlockSpec(memory_space=pl.ANY)] * 2,
            out_specs=[pl.BlockSpec(memory_space=pltpu.VMEM)] * 2,
            scratch_shapes=[
                pltpu.VMEM((2, 2, rows, half * block), jnp.float32),
                pltpu.VMEM((2, 2, half, block, rows), jnp.float32),
                pltpu.VMEM((2, n, block, rows), jnp.float32),
                pltpu.SemaphoreType.DMA((2, 2)),
                pltpu.SemaphoreType.DMA((2, 2, half)),
                pltpu.SemaphoreType.DMA((2, n)),
            ],
            compiler_params=pltpu.CompilerParams(collective_id=0, has_side_effects=True),
            name="exchange",
        )(samples_in, second_samples_in)
        return first.T, second.T

    placed = (P("batch", "group"), P("batch", "group"))
    return jax.shard_map(
        shards,
        mesh=mesh,
        in_specs=placed,
        out_specs=(P(None, ("group", "batch")), P(None, ("group", "batch"))),
        check_vma=False,
    )
```

time: 33.3 us -> 22.8 us (0.68)
  Pallas kernels: 0 us -> 19.5 us
  waiting for transfers between devices: 17.3 us -> 0 us
  starting transfers between devices: 11.1 us -> 0 us
  other arithmetic: 1.22 us -> 0 us
    pallas_call x0 -> x1, Pallas kernels: none -> 19.5 us  [shards(): pl.pallas_call(functools.partial(kernel, n), out_shape=(out, out), in_spe...]
    all_to_all x2 -> x0, waiting for transfers between devices: 17.3 us -> none  [the longest x1 9.25 us: shards(): lax.all_to_all(second_samples_in, 'batch', split_axis=1, concat_axis=0, t...]
    all_to_all x2 -> x0, starting transfers between devices: 11.1 us -> none  [the longest x1 7.47 us: shards(): lax.all_to_all(samples_in, 'batch', split_axis=1, concat_axis=0, tiled=True)]
    div x3 -> x0, other arithmetic: 0.93 us -> none  [the longest x1 0.91 us: shards(): (wide_second_standard - low_second_standard) / (high_second_standard - lo...]
  transfers between devices with their start and end apart: 2 -> 0, of which waited for: 2 -> 0; matrix products, arithmetic and copies ran while one was open for 3% -> 0% of each run, Pallas kernels for 0% -> 0%
where the time goes in v1:
time: 22.8 us; the launch traced here: 22.6 us
  Pallas kernels  19.5 us (86%)
  local copies, waits for them, and re-layouts  2.42 us (11%)
  between operations  0.65 us (3%)
    pallas_call x1, Pallas kernels, shards(): pl.pallas_call(functools.partial(kernel, n), out_shape=(out, out), in_spe...  19.5 us
    unnamed x4, local copies, waits for them, and re-layouts  2.42 us

profile of v1, /device:TPU:0, one launch (start us, length us, event | category | flops | bytes accessed | tf_op | source)
XLA Modules:
  0.0 22.6 jit_solution(5668386876751657282)
XLA Ops:
  0.6 19.5 %exchange.1 = (f32[32,2048]{1,0:T(8,128)}, f32[32,2048]{1,0:T(8,128)}) custom-call(f32[256,256]{1,0:T(8,128)} %first_hbm.1, f32[256,256]{1,0:T(8,128)} %second_hbm.1), custom_call_target="tpu_custom_call" | custom-call | tf_op jit(solution)/shard_map/exchange/pallas_call | solution.py:153
  20.2 0.0 copy-start
  20.2 1.7 %copy.6 = f32[2048,32]{0,1:T(8,128)} copy(f32[2048,32]{0,1:T(8,128)} %bitcast.3) | data formatting | bytes 524288
  21.9 0.0 copy-done
  21.9 0.7 %copy.7 = f32[2048,32]{0,1:T(8,128)} copy(f32[2048,32]{0,1:T(8,128)S(1)} %bitcast.2) | data formatting | bytes 524288
Async XLA Ops:
  20.2 1.7 %copy-start = (f32[32,2048]{1,0:T(8,128)S(1)}, f32[32,2048]{1,0:T(8,128)}, u32[]{:S(2)}) copy-start(f32[32,2048]{1,0:T(8,128)} %get-tuple-element.5) | copy-start | bytes 786436

commit v2 on v1

--- a/solution.py
+++ b/solution.py
@@ -19,9 +19,8 @@
     return lax.fori_loop(0, count, body, init)
 
 
-def kernel(n, first_hbm, second_hbm, first_out, second_out, raw, turned, got, load_sem, send_sem, recv_sem):
+def kernel(n, first_hbm, second_hbm, got, total, raw, turned, load_sem, send_sem, recv_sem):
     ins = (first_hbm, second_hbm)
-    outs = (first_out, second_out)
     rows, width = first_hbm.shape
     block = width // n
     half = n // 2
@@ -117,29 +116,51 @@
             sums[a] = loop(half - side, take, sums[a])
 
     for a in range(2):
-        low, high = (jnp.sum(s, axis=1, keepdims=True) / (n * rows) for s in sums[a])
+        for kind in range(2):
+            total[a, kind] = sums[a][kind]
+
+    for side in range(2):
+        for a in range(2):
+
+            def drain(step, carry, side=side, a=a):
+                send(side, a, step + side).wait_send()
+                return carry
+
+            loop(half - side, drain, 0)
+
+
+def rescale(got, total, first_out, second_out, ready, store_sem):
+    _, n, block, rows = got.shape
+    outs = (first_out, second_out)
+    pieces = min(n, 4)
+    each = n // pieces
+    copies = []
+    for a in range(2):
+        low, high = (
+            jnp.sum(total[a, kind], axis=1, keepdims=True) / (n * rows) for kind in range(2)
+        )
         scale = 1.0 / (high - low + 0.1)
         low = jnp.broadcast_to(low, (block, rows))
         scale = jnp.broadcast_to(scale, (block, rows))
-        out = outs[a]
-
-        def rescale(source, carry, a=a, out=out, low=low, scale=scale):
-            start = source * rows
-            if not isinstance(start, int):
-                start = pl.multiple_of(start, LANES)
-            out[:, pl.ds(start, rows)] = (got[a, source] - low) * scale
-            return carry
-
-        loop(n, rescale, 0)
-
-    for side in range(2):
-        for a in range(2):
-
-            def drain(step, carry, side=side, a=a):
-                send(side, a, step + side).wait_send()
+        for piece in range(pieces):
+
+            def turn(step, carry, a=a, piece=piece, low=low, scale=scale):
+                source = piece * each + step
+                start = source * rows
+                if not isinstance(start, int):
+                    start = pl.multiple_of(start, LANES)
+                ready[a, :, pl.ds(start, rows)] = (got[a, source] - low) * scale
                 return carry
 
-            loop(half - side, drain, 0)
+            loop(each, turn, 0)
+            part = pl.ds(piece * each * rows, each * rows)
+            copy = pltpu.make_async_copy(
+                ready.at[a, :, part], outs[a].at[:, part], store_sem.at[a, piece]
+            )
+            copy.start()
+            copies.append(copy)
+    for copy in copies:
+        copy.wait()
 
 
 def solution(mesh):
@@ -149,23 +170,46 @@
         rows, width = samples_in.shape
         block = width // n
         half = n // 2
-        out = jax.ShapeDtypeStruct((block, n * rows), jnp.float32)
-        first, second = pl.pallas_call(
+        held = 2 * rows * width * 4
+        got, total = pl.pallas_call(
             functools.partial(kernel, n),
-            out_shape=(out, out),
-            in_specs=[pl.BlockSpec(memory_space=pl.ANY)] * 2,
+            out_shape=(
+                pltpu.VMEM((2, n, block, rows), jnp.float32),
+                pltpu.VMEM((2, 2, block, LANES), jnp.float32),
+            ),
+            in_specs=[pl.BlockSpec(memory_space=pltpu.HBM)] * 2,
             out_specs=[pl.BlockSpec(memory_space=pltpu.VMEM)] * 2,
             scratch_shapes=[
                 pltpu.VMEM((2, 2, rows, half * block), jnp.float32),
                 pltpu.VMEM((2, 2, half, block, rows), jnp.float32),
-                pltpu.VMEM((2, n, block, rows), jnp.float32),
                 pltpu.SemaphoreType.DMA((2, 2)),
                 pltpu.SemaphoreType.DMA((2, 2, half)),
                 pltpu.SemaphoreType.DMA((2, n)),
             ],
-            compiler_params=pltpu.CompilerParams(collective_id=0, has_side_effects=True),
+            compiler_params=pltpu.CompilerParams(
+                collective_id=0, has_side_effects=True, vmem_limit_bytes=4 * held + (8 << 20)
+            ),
             name="exchange",
-        )(samples_in, second_samples_in)
+        )(
+            pltpu.with_memory_space_constraint(samples_in, pltpu.HBM),
+            pltpu.with_memory_space_constraint(second_samples_in, pltpu.HBM),
+        )
+        out = jax.ShapeDtypeStruct((block, n * rows), jnp.float32)
+        first, second = pl.pallas_call(
+            rescale,
+            out_shape=(out, out),
+            in_specs=[pl.BlockSpec(memory_space=pltpu.VMEM)] * 2,
+            out_specs=[pl.BlockSpec(memory_space=pl.ANY)] * 2,
+            scratch_shapes=[
+                pltpu.VMEM((2, block, n * rows), jnp.float32),
+                pltpu.SemaphoreType.DMA((2, min(n, 4))),
+            ],
+            compiler_params=pltpu.CompilerParams(vmem_limit_bytes=2 * held + (8 << 20)),
+            name="rescale",
+        )(
+            pltpu.with_memory_space_constraint(got, pltpu.VMEM),
+            pltpu.with_memory_space_constraint(total, pltpu.VMEM),
+        )
         return first.T, second.T
 
     placed = (P("batch", "group"), P("batch", "group"))

time: 22.8 us -> 20.4 us (0.89)
  local copies, waits for them, and re-layouts: 2.42 us -> 0 us
    unnamed x4 -> x0, local copies, waits for them, and re-layouts: 2.42 us -> none
    pallas_call x1 -> x2, Pallas kernels: 19.5 us -> 19.6 us  [the longest x1 18.6 us: shards(): pl.pallas_call(functools.partial(kernel, n), out_shape=(pltpu.VMEM((2, n,...]
where the time goes in v2:
time: 20.4 us; the launch traced here: 20.2 us
  Pallas kernels  19.6 us (96%)
  between operations  0.64 us (3%)
    pallas_call x1, Pallas kernels, shards(): pl.pallas_call(functools.partial(kernel, n), out_shape=(pltpu.VMEM((2, n,...  18.6 us
    pallas_call x1, Pallas kernels, shards(): pl.pallas_call(rescale, out_shape=(out, out), in_specs=[pl.BlockSpec(memo...  0.97 us

profile of v2, /device:TPU:0, one launch (start us, length us, event | category | flops | bytes accessed | tf_op | source)
XLA Modules:
  0.0 20.2 jit_solution(1390313745405401319)
XLA Ops:
  0.6 18.6 %exchange.1 = (f32[2,8,32,256]{3,2,1,0:T(8,128)S(1)}, f32[2,2,32,128]{3,2,1,0:T(8,128)S(1)}) custom-call(f32[256,256]{1,0:T(8,128)} %first_hbm.1, f32[256,256]{1,0:T(8,128)} %second_hbm.1), custom_call_target="tpu_custom_call" | custom-call | tf_op jit(solution)/shard_map/exchange/pallas_call | solution.py:174
  19.3 1.0 %rescale.1 = (f32[32,2048]{1,0:T(8,128)}, f32[32,2048]{1,0:T(8,128)}) custom-call(f32[2,8,32,256]{3,2,1,0:T(8,128)S(1)} %get-tuple-element.6.got, f32[2,2,32,128]{3,2,1,0:T(8,128)S(1)} %get-tuple-element.7.total), custom_call_target="tpu_custom_call" | custom-call | tf_op jit(solution)/shard_map/rescale/pallas_call | solution.py:198

commit v3 on v2

--- a/solution.py
+++ b/solution.py
@@ -19,20 +19,17 @@
     return lax.fori_loop(0, count, body, init)
 
 
-def kernel(n, first_hbm, second_hbm, got, total, raw, turned, load_sem, send_sem, recv_sem):
+def kernel(n, first_hbm, second_hbm, got, total, raw, turned, load_sem, send_sem, recv_sem, here):
     ins = (first_hbm, second_hbm)
     rows, width = first_hbm.shape
     block = width // n
-    half = n // 2
+    half, quarter = n // 2, n // 4
     span = half * block
     me = lax.axis_index("batch")
-    mine, place = me // half, me % half
-    sides = ((mine + 1) % 2, mine)
 
     def load(side, a):
-        start = pl.multiple_of(sides[side] * span, span)
         return pltpu.make_async_copy(
-            ins[a].at[:, pl.ds(start, span)], raw.at[a, side], load_sem.at[a, side]
+            ins[a].at[:, side * span : (side + 1) * span], raw.at[a, side], load_sem.at[a, side]
         )
 
     for side in range(2):
@@ -41,55 +38,82 @@
 
     barrier = pltpu.get_barrier_semaphore()
 
-    def greet(step, carry):
+    def greet(target, carry):
         pl.semaphore_signal(
-            barrier, inc=1, device_id={"batch": (me + 1 + step) % n}, device_id_type=MESH
+            barrier, inc=1, device_id={"batch": target}, device_id_type=MESH
         )
         return carry
 
-    loop(n - 1, greet, 0)
-
-    def send(side, a, step):
-        spot = (place + step) % half
+    lax.fori_loop(me + 1, n, greet, 0)
+
+    def send(a, target):
         return pltpu.make_async_remote_copy(
-            src_ref=turned.at[a, side, spot],
+            src_ref=turned.at[a, target],
             dst_ref=got.at[a, me],
-            send_sem=send_sem.at[a, side, step],
+            send_sem=send_sem.at[a, target],
             recv_sem=recv_sem.at[a, me],
-            device_id={"batch": sides[side] * half + spot},
+            device_id={"batch": target},
             device_id_type=MESH,
         )
 
-    def arrival(side, a, step):
-        source = sides[side] * half + (place - step + half) % half
-        copy = pltpu.make_async_remote_copy(
-            src_ref=turned.at[a, side, 0],
+    def arrival(a, source):
+        return pltpu.make_async_remote_copy(
+            src_ref=turned.at[a, source],
             dst_ref=got.at[a, source],
-            send_sem=send_sem.at[a, side, step],
+            send_sem=send_sem.at[a, source],
             recv_sem=recv_sem.at[a, source],
             device_id={"batch": source},
             device_id_type=MESH,
         )
-        return source, copy
-
-    greeted = False
-    for side in range(2):
-        for a in range(2):
-            load(side, a).wait()
-            for start in range(0, span, LANES):
-                tile = raw[a, side, :, start : start + LANES].T
-                turned[a, side, start // block : (start + LANES) // block] = tile.reshape(
-                    LANES // block, block, rows
-                )
-            if not greeted:
-                pl.semaphore_wait(barrier, n - 1)
-                greeted = True
-
-            def push(step, carry, side=side, a=a):
-                send(side, a, step + side).start()
-                return carry
-
-            loop(half - side, push, 0)
+
+    def transpose(side, a):
+        load(side, a).wait()
+        for start in range(0, span, LANES):
+            tile = raw[a, side, :, start : start + LANES].T
+            spot = side * half + start // block
+            turned[a, spot : spot + LANES // block] = tile.reshape(LANES // block, block, rows)
+
+    def push(a, first):
+        def one(step, carry):
+            target = first + step
+
+            @pl.when(target != me)
+            def _():
+                if a == 0:
+
+                    @pl.when(target > me)
+                    def _():
+                        pl.semaphore_wait(here.at[target], 1)
+
+                send(a, target).start()
+
+            return carry
+
+        loop(quarter, one, 0)
+
+    transpose(0, 0)
+
+    @pl.when(me > 0)
+    def _():
+        pl.semaphore_wait(barrier, me)
+
+    def announce(target, carry):
+        pl.semaphore_signal(
+            here.at[me], inc=1, device_id={"batch": target}, device_id_type=MESH
+        )
+        return carry
+
+    lax.fori_loop(0, me, announce, 0)
+    push(0, 0)
+    transpose(0, 1)
+    push(1, 0)
+    push(0, quarter)
+    push(1, quarter)
+    transpose(1, 0)
+    transpose(1, 1)
+    for first in (half, half + quarter):
+        push(0, first)
+        push(1, first)
 
     def add(sums, values):
         low, high = sums
@@ -100,33 +124,31 @@
         return low, high
 
     zero = jnp.zeros((block, LANES), jnp.float32)
-    sums = []
     for a in range(2):
-        own = turned[a, 1, place]
-        got[a, me] = own
-        sums.append(add((zero, zero), own))
-    for side in range(2):
-        for a in range(2):
-
-            def take(step, carry, side=side, a=a):
-                source, copy = arrival(side, a, step + side)
-                copy.wait_recv()
-                return add(carry, got[a, source])
-
-            sums[a] = loop(half - side, take, sums[a])
-
+        got[a, me] = turned[a, me]
+
+    def take(source, sums):
+        @pl.when(source != me)
+        def _():
+            for a in range(2):
+                arrival(a, source).wait_recv()
+
+        return tuple(add(sums[a], got[a, source]) for a in range(2))
+
+    sums = loop(n, take, ((zero, zero), (zero, zero)))
     for a in range(2):
         for kind in range(2):
             total[a, kind] = sums[a][kind]
 
-    for side in range(2):
-        for a in range(2):
-
-            def drain(step, carry, side=side, a=a):
-                send(side, a, step + side).wait_send()
-                return carry
-
-            loop(half - side, drain, 0)
+    def drain(target, carry):
+        @pl.when(target != me)
+        def _():
+            for a in range(2):
+                send(a, target).wait_send()
+
+        return carry
+
+    loop(n, drain, 0)
 
 
 def rescale(got, total, first_out, second_out, ready, store_sem):
@@ -181,10 +203,11 @@
             out_specs=[pl.BlockSpec(memory_space=pltpu.VMEM)] * 2,
             scratch_shapes=[
                 pltpu.VMEM((2, 2, rows, half * block), jnp.float32),
-                pltpu.VMEM((2, 2, half, block, rows), jnp.float32),
+                pltpu.VMEM((2, n, block, rows), jnp.float32),
                 pltpu.SemaphoreType.DMA((2, 2)),
-                pltpu.SemaphoreType.DMA((2, 2, half)),
                 pltpu.SemaphoreType.DMA((2, n)),
+                pltpu.SemaphoreType.DMA((2, n)),
+                pltpu.SemaphoreType.REGULAR((n,)),
             ],
             compiler_params=pltpu.CompilerParams(
                 collective_id=0, has_side_effects=True, vmem_limit_bytes=4 * held + (8 << 20)

time: 20.4 us -> 17.8 us (0.87)
  Pallas kernels: 19.6 us -> 16.8 us
    pallas_call x1, Pallas kernels: 18.6 us -> 15.9 us  [shards(): pl.pallas_call(functools.partial(kernel, n), out_shape=(pltpu.VMEM((2, n,...]
where the time goes in v3:
time: 17.8 us; the launch traced here: 17.5 us
  Pallas kernels  16.8 us (94%)
  between operations  0.64 us (4%)
    pallas_call x1, Pallas kernels, shards(): pl.pallas_call(functools.partial(kernel, n), out_shape=(pltpu.VMEM((2, n,...  15.9 us
    pallas_call x1, Pallas kernels, shards(): pl.pallas_call(rescale, out_shape=(out, out), in_specs=[pl.BlockSpec(memo...  0.97 us

profile of v3, /device:TPU:0, one launch (start us, length us, event | category | flops | bytes accessed | tf_op | source)
XLA Modules:
  0.0 17.5 jit_solution(15435782667598929622)
XLA Ops:
  0.6 15.9 %exchange.1 = (f32[2,8,32,256]{3,2,1,0:T(8,128)S(1)}, f32[2,2,32,128]{3,2,1,0:T(8,128)S(1)}) custom-call(f32[256,256]{1,0:T(8,128)} %first_hbm.1, f32[256,256]{1,0:T(8,128)} %second_hbm.1), custom_call_target="tpu_custom_call" | custom-call | tf_op jit(solution)/shard_map/exchange/pallas_call | solution.py:196
  16.5 1.0 %rescale.1 = (f32[32,2048]{1,0:T(8,128)}, f32[32,2048]{1,0:T(8,128)}) custom-call(f32[2,8,32,256]{3,2,1,0:T(8,128)S(1)} %get-tuple-element.6.got, f32[2,2,32,128]{3,2,1,0:T(8,128)S(1)} %get-tuple-element.7.total), custom_call_target="tpu_custom_call" | custom-call | tf_op jit(solution)/shard_map/rescale/pallas_call | solution.py:221

commit v4 on v3

--- a/solution.py
+++ b/solution.py
@@ -73,7 +73,7 @@
             spot = side * half + start // block
             turned[a, spot : spot + LANES // block] = tile.reshape(LANES // block, block, rows)
 
-    def push(a, first):
+    def push(a, first, count):
         def one(step, carry):
             target = first + step
 
@@ -89,9 +89,8 @@
 
             return carry
 
-        loop(quarter, one, 0)
-
-    transpose(0, 0)
+        loop(count, one, 0)
+
 
     @pl.when(me > 0)
     def _():
@@ -104,16 +103,19 @@
         return carry
 
     lax.fori_loop(0, me, announce, 0)
-    push(0, 0)
+    transpose(0, 0)
     transpose(0, 1)
-    push(1, 0)
-    push(0, quarter)
-    push(1, quarter)
+    push(0, 0, 1)
+    push(1, 0, 1)
+    push(0, 1, quarter - 1)
+    push(1, 1, quarter - 1)
+    push(0, quarter, quarter)
+    push(1, quarter, quarter)
     transpose(1, 0)
     transpose(1, 1)
     for first in (half, half + quarter):
-        push(0, first)
-        push(1, first)
+        push(0, first, quarter)
+        push(1, first, quarter)
 
     def add(sums, values):
         low, high = sums

time: 17.8 us -> 17.5 us (0.983)
  the two profiles are of different devices: /device:TPU:0 before, /device:TPU:24 now
where the time goes in v4:
time: 17.5 us; the launch traced here: 17.4 us
  Pallas kernels  16.8 us (96%)
  between operations  0.64 us (4%)
    pallas_call x1, Pallas kernels, shards(): pl.pallas_call(functools.partial(kernel, n), out_shape=(pltpu.VMEM((2, n,...  15.8 us
    pallas_call x1, Pallas kernels, shards(): pl.pallas_call(rescale, out_shape=(out, out), in_specs=[pl.BlockSpec(memo...  0.97 us

profile of v4, /device:TPU:24, one launch (start us, length us, event | category | flops | bytes accessed | tf_op | source)
XLA Modules:
  0.0 17.4 jit_solution(7520184395919504161)
XLA Ops:
  0.6 15.8 %exchange.1 = (f32[2,8,32,256]{3,2,1,0:T(8,128)S(1)}, f32[2,2,32,128]{3,2,1,0:T(8,128)S(1)}) custom-call(f32[256,256]{1,0:T(8,128)} %first_hbm.1, f32[256,256]{1,0:T(8,128)} %second_hbm.1), custom_call_target="tpu_custom_call" | custom-call | tf_op jit(solution)/shard_map/exchange/pallas_call | solution.py:198
  16.4 1.0 %rescale.1 = (f32[32,2048]{1,0:T(8,128)}, f32[32,2048]{1,0:T(8,128)}) custom-call(f32[2,8,32,256]{3,2,1,0:T(8,128)S(1)} %get-tuple-element.6.got, f32[2,2,32,128]{3,2,1,0:T(8,128)S(1)} %get-tuple-element.7.total), custom_call_target="tpu_custom_call" | custom-call | tf_op jit(solution)/shard_map/rescale/pallas_call | solution.py:223

commit v5 on v4

--- a/solution.py
+++ b/solution.py
@@ -23,7 +23,7 @@
     ins = (first_hbm, second_hbm)
     rows, width = first_hbm.shape
     block = width // n
-    half, quarter = n // 2, n // 4
+    half = n // 2
     span = half * block
     me = lax.axis_index("batch")
 
@@ -73,24 +73,22 @@
             spot = side * half + start // block
             turned[a, spot : spot + LANES // block] = tile.reshape(LANES // block, block, rows)
 
-    def push(a, first, count):
+    def push(first, count):
         def one(step, carry):
             target = first + step
 
+            @pl.when(target > me)
+            def _():
+                pl.semaphore_wait(here.at[target], 1)
+
             @pl.when(target != me)
             def _():
-                if a == 0:
-
-                    @pl.when(target > me)
-                    def _():
-                        pl.semaphore_wait(here.at[target], 1)
-
-                send(a, target).start()
+                for a in range(2):
+                    send(a, target).start()
 
             return carry
 
         loop(count, one, 0)
-
 
     @pl.when(me > 0)
     def _():
@@ -105,17 +103,10 @@
     lax.fori_loop(0, me, announce, 0)
     transpose(0, 0)
     transpose(0, 1)
-    push(0, 0, 1)
-    push(1, 0, 1)
-    push(0, 1, quarter - 1)
-    push(1, 1, quarter - 1)
-    push(0, quarter, quarter)
-    push(1, quarter, quarter)
+    push(0, half)
     transpose(1, 0)
     transpose(1, 1)
-    for first in (half, half + quarter):
-        push(0, first, quarter)
-        push(1, first, quarter)
+    push(half, half)
 
     def add(sums, values):
         low, high = sums

time: 17.5 us -> 17.3 us (0.989)
  Pallas kernels: 16.8 us -> 16.5 us
    pallas_call x1, Pallas kernels: 15.8 us -> 15.6 us  [shards(): pl.pallas_call(functools.partial(kernel, n), out_shape=(pltpu.VMEM((2, n,...]
where the time goes in v5:
time: 17.3 us; the launch traced here: 17.2 us
  Pallas kernels  16.5 us (95%)
  between operations  0.64 us (4%)
    pallas_call x1, Pallas kernels, shards(): pl.pallas_call(functools.partial(kernel, n), out_shape=(pltpu.VMEM((2, n,...  15.6 us
    pallas_call x1, Pallas kernels, shards(): pl.pallas_call(rescale, out_shape=(out, out), in_specs=[pl.BlockSpec(memo...  0.97 us

profile of v5, /device:TPU:24, one launch (start us, length us, event | category | flops | bytes accessed | tf_op | source)
XLA Modules:
  0.0 17.2 jit_solution(4332986736199749784)
XLA Ops:
  0.6 15.6 %exchange.1 = (f32[2,8,32,256]{3,2,1,0:T(8,128)S(1)}, f32[2,2,32,128]{3,2,1,0:T(8,128)S(1)}) custom-call(f32[256,256]{1,0:T(8,128)} %first_hbm.1, f32[256,256]{1,0:T(8,128)} %second_hbm.1), custom_call_target="tpu_custom_call" | custom-call | tf_op jit(solution)/shard_map/exchange/pallas_call | solution.py:189
  16.2 1.0 %rescale.1 = (f32[32,2048]{1,0:T(8,128)}, f32[32,2048]{1,0:T(8,128)}) custom-call(f32[2,8,32,256]{3,2,1,0:T(8,128)S(1)} %get-tuple-element.6.got, f32[2,2,32,128]{3,2,1,0:T(8,128)S(1)} %get-tuple-element.7.total), custom_call_target="tpu_custom_call" | custom-call | tf_op jit(solution)/shard_map/rescale/pallas_call | solution.py:214
